TPU v7x, 256 devices: a whole 4x4x8 slice. The times are simulated.
256 devices in a mesh: dp: 8 (over x, y_lo), expert: 16 (over z, core), tensor: 2 (over y_hi).
Axes of the slice: x: 4, y: 4 (y_hi: 2, y_lo: 2; y = y_hi * 2 + y_lo), z: 8, core: 2. Of those that a mesh axis runs over, the one named last changes fastest.
Arguments:
- tokens: bfloat16 [1536, 256, 1280], P(('dp', 'expert', 'tensor')), may hold values from -16 to 16
- cotangent: bfloat16 [1536, 256, 1280], P(('dp', 'expert', 'tensor')), may hold values from -6 to 6
- norm_gain: float32 [1280], replicated, may hold values from 0.5 to 1.5
- slot_keys: bfloat16 [1280, 32], replicated, may hold values from -2 to 2
- w_in: bfloat16 [16, 1280, 2560], P('expert', None, 'tensor'), may hold values from -0.15625 to 0.15625
- w_out: bfloat16 [16, 2560, 1280], P('expert', 'tensor'), may hold values from -0.125 to 0.125
Outputs:
- grad_tokens: bfloat16 [1536, 256, 1280], P(('dp', 'expert', 'tensor'))
- grad_gain: float32 [1280], replicated
- grad_keys: float32 [1280, 32], replicated
- grad_in: bfloat16 [16, 1280, 2560], P('expert', 'dp', 'tensor')
- grad_out: bfloat16 [16, 2560, 1280], P('expert', 'tensor', 'dp')
All inputs are finite; a program needn't handle non-finite values.
Results may differ from a plain program's by a relative error of at most 0.014.
The roundings to bfloat16 on the way count: a program that leaves them out, or rounds other values in their place, can miss the bound.
Values may be sent and summed in bfloat16 or wider, within the bound.
No kernel may reach another device: no remote copies, remote signals or barrier semaphores. Data moves between devices by JAX's collectives and lax.ppermute only.
A program may use at most 128 MiB of HBM per device.

v0:
```python
import jax
import jax.numpy as jnp
from jax import lax
from jax.sharding import PartitionSpec as P

SLOT_PER = 2
EPSILON = 1e-06
ROWS = 24
LANES = 128


def from_everyone(shard, axis):
    devices = lax.axis_size(axis)
    return lax.all_to_all(
        jnp.broadcast_to(shard[None], (devices, *shard.shape)), axis, 0, 0, tiled=True
    )


def swapped(value):
    return lax.ppermute(value, "tensor", [(0, 1), (1, 0)])


def mixing_forward(tokens, gain, slot_keys):
    average = jnp.mean(tokens, axis=-1, keepdims=True, dtype=jnp.float32)
    centred = tokens.astype(jnp.float32) - average
    spread = jnp.mean(centred * centred, axis=-1, keepdims=True)
    inverse = lax.rsqrt(spread + EPSILON)
    scaled = centred * inverse
    normed = (scaled * gain).astype(jnp.bfloat16)
    logits = jnp.einsum("bmd,dn->bmn", normed, slot_keys, preferred_element_type=jnp.float32)
    dispatch = jax.nn.softmax(logits, axis=1)
    combine = jax.nn.softmax(logits, axis=2)
    dispatch_low = dispatch.astype(jnp.bfloat16)
    slot_values = jnp.einsum(
        "bmn,bmd->bnd", dispatch_low, normed, preferred_element_type=jnp.float32
    )
    return (slot_values, combine, (scaled, inverse, normed, dispatch, combine, dispatch_low))


def split_wide(value):
    high = value.astype(jnp.bfloat16)
    low = (value - high.astype(jnp.float32)).astype(jnp.bfloat16)
    return (high, low)


def contract_rows(left, right):
    return lax.dot_general(
        left, right, (((0,), (0,)), ((), ())), preferred_element_type=jnp.float32
    )


def contract_cols(left, right):
    return lax.dot_general(
        left, right, (((1,), (1,)), ((), ())), preferred_element_type=jnp.float32
    )


def summed_everywhere(keys_term, gain_part):
    slots, features = keys_term.shape
    blocks = features // LANES
    group = lax.axis_size("expert")
    flat = jnp.concatenate(
        [
            keys_term.reshape(slots, blocks, LANES).transpose(1, 0, 2).reshape(-1, LANES),
            gain_part.reshape(blocks, LANES),
            jnp.zeros((group * ROWS - (slots + 1) * blocks, LANES), jnp.float32),
        ]
    ).reshape(group, ROWS, LANES)
    mine = jnp.sum(lax.all_to_all(flat, "expert", 0, 0, tiled=True), axis=0)
    mine = jnp.sum(from_everyone(mine, ("dp", "tensor")), axis=0)
    whole = from_everyone(mine, "expert").reshape(-1, LANES)
    keys_sum = whole[: slots * blocks].reshape(blocks, slots, LANES).transpose(1, 0, 2)
    return (keys_sum.reshape(slots, features), whole[slots * blocks :][:blocks].reshape(-1))


def local(tokens, cotangent, norm_gain, slot_keys, w_in, w_out):
    local_imgs, token_count, features = tokens.shape
    slot_count = slot_keys.shape[1]
    experts = slot_count // SLOT_PER
    slot_values, combine, saved = mixing_forward(tokens, norm_gain, slot_keys)
    slot_low = slot_values.astype(jnp.bfloat16)
    slot_inputs = slot_low.reshape(local_imgs, experts, SLOT_PER, features)
    arrived = lax.all_to_all(slot_inputs, "expert", split_axis=1, concat_axis=0, tiled=True)
    own = arrived.reshape(-1, features)
    half = own.shape[0]
    slot_rows = jnp.concatenate([own, swapped(own)])
    combine_low = combine.astype(jnp.bfloat16)
    grad_slots = jnp.einsum(
        "bmn,bmd->bnd", combine_low, cotangent, preferred_element_type=jnp.float32
    )
    grad_slots = grad_slots.astype(jnp.bfloat16).reshape(local_imgs, experts, SLOT_PER, features)
    grads_sent = lax.all_to_all(grad_slots, "expert", split_axis=1, concat_axis=0, tiled=True)
    own_grads = grads_sent.reshape(-1, features)
    grad_rows = jnp.concatenate([own_grads, swapped(own_grads)])
    first_proj = w_in[0]
    second_proj = w_out[0]
    pre_act = jnp.dot(slot_rows, first_proj, preferred_element_type=jnp.float32)
    hidden = jax.nn.gelu(pre_act).astype(jnp.bfloat16)

    def reduced_and_returned(partial):
        theirs = swapped(partial[half:].astype(jnp.bfloat16))
        total = (partial[:half] + theirs.astype(jnp.float32)).astype(jnp.bfloat16)
        return lax.all_to_all(
            total.reshape(arrived.shape), "expert", split_axis=0, concat_axis=1, tiled=True
        ).reshape(local_imgs, slot_count, features)

    returned = reduced_and_returned(
        jnp.dot(hidden, second_proj, preferred_element_type=jnp.float32)
    )
    grad_hidden = contract_cols(grad_rows, second_proj)
    grad_pre = jax.vjp(jax.nn.gelu, pre_act)[1](grad_hidden)[0].astype(jnp.bfloat16)
    grad_back = reduced_and_returned(contract_cols(grad_pre, first_proj))
    second_part = contract_rows(grad_rows, hidden).astype(jnp.bfloat16)
    first_part = contract_rows(slot_rows, grad_pre).astype(jnp.bfloat16)
    grad_second = lax.psum_scatter(second_part, "dp", scatter_dimension=0, tiled=True)
    grad_first = lax.psum_scatter(first_part, "dp", scatter_dimension=0, tiled=True)
    returned, grad_back, second_part, first_part = lax.optimization_barrier(
        (returned, grad_back, second_part, first_part)
    )
    scaled, inverse, normed, dispatch, combine, dispatch_low = saved
    combine_grad = jnp.einsum(
        "bmd,bnd->bmn", cotangent, returned, preferred_element_type=jnp.float32
    )
    grad_dispatch = jnp.einsum(
        "bnd,bmd->bmn", grad_back, normed, preferred_element_type=jnp.float32
    )
    grad_logits = dispatch * (
        grad_dispatch - jnp.sum(dispatch * grad_dispatch, axis=1, keepdims=True)
    )
    grad_logits = grad_logits + combine * (
        combine_grad - jnp.sum(combine * combine_grad, axis=2, keepdims=True)
    )
    high, low = split_wide(grad_logits)
    pair = jnp.concatenate([high, low], axis=2)
    keys_pair = jnp.einsum("bmn,bmd->nd", pair, normed, preferred_element_type=jnp.float32)
    keys_term = keys_pair[:slot_count] + keys_pair[slot_count:]
    gain_part = jnp.sum(grad_back.astype(jnp.float32) * slot_low.astype(jnp.float32), axis=(0, 1))
    keys_sum, gain_sum = summed_everywhere(keys_term, gain_part)
    keys_wide = slot_keys.astype(jnp.float32)
    grad_keys = keys_sum.T
    grad_gain = (gain_sum + jnp.sum(keys_wide * grad_keys, axis=1)) / norm_gain
    weights = jnp.concatenate([dispatch_low, pair], axis=2)
    keys_rows = jnp.broadcast_to(slot_keys.T[None], (local_imgs, slot_count, features))
    values = jnp.concatenate([grad_back, keys_rows, keys_rows], axis=1)
    grad_normed = jnp.einsum("bmn,bnd->bmd", weights, values, preferred_element_type=jnp.float32)
    grad_scaled = grad_normed * norm_gain
    first_mean = jnp.mean(grad_scaled, axis=-1, keepdims=True)
    second_mean = jnp.mean(grad_scaled * scaled, axis=-1, keepdims=True)
    grad_tok = inverse * (grad_scaled - first_mean - scaled * second_mean)
    grad_tokens = (cotangent.astype(jnp.float32) + grad_tok).astype(jnp.bfloat16)
    return (grad_tokens, grad_gain, grad_keys, grad_first[None], grad_second.T[None])


def solution(mesh):
    placed = (
        P(("dp", "expert", "tensor"), None, None),
        P(("dp", "expert", "tensor"), None, None),
        P(),
        P(),
        P("expert", None, "tensor"),
        P("expert", "tensor", None),
    )
    return jax.shard_map(
        local,
        mesh=mesh,
        in_specs=placed,
        out_specs=(
            P(("dp", "expert", "tensor"), None, None),
            P(),
            P(),
            P("expert", "dp", "tensor"),
            P("expert", "tensor", "dp"),
        ),
        check_vma=False,
    )
```

profile of v0, /device:TPU:11, one launch (start us, length us, event | category | flops | bytes accessed | tf_op | source)
XLA Modules:
  0.0 266.0 jit_solution(17931824056655264525)
XLA Ops:
  7.2 2.8 %convert_reduce_fusion = f32[6,256]{1,0:T(8,128)S(1)} fusion(bf16[6,256,1280]{2,1,0:T(8,128)(2,1)} %param.6), kind=kLoop, calls=%fused_computation.5 | loop fusion | flops 3930624 | bytes 3938304 | tf_op jit(solution)/shard_map/reduce_sum | solution.py:24
  11.8 1.7 fusion.61
  16.0 2.4 convolution_convert_fusion.3
  18.4 2.0 reshape.92
  20.4 2.2 copy.26
  22.6 9.2 %all-to-all-start = ((bf16[6,16,2,1280]{3,2,0,1:T(2,128)(2,1)}), bf16[6,16,2,1280]{3,2,0,1:T(2,128)(2,1)}, u32[]{:S(2)}, u32[]{:S(2)}) async-start(bf16[6,16,2,1280]{3,2,0,1:T(2,128)(2,1)} %copy.26), calls=%async_computation | async-start | bytes 983040 | tf_op jit(solution)/shard_map/all_to_all | solution.py:83
  32.5 3.6 %convolution_convert_fusion.2 = bf16[6,32,1280]{2,1,0:T(8,128)(2,1)} fusion(bf16[6,256,1280]{2,1,0:T(8,128)(2,1)} %param.7, f32[6,256]{1,0:T(8,128)S(1)} %get-tuple-element.17, f32[6,256,32]{1,2,0:T(8,128)S(1)} %fusion.61), kind=kOutput, calls=%fused_computation.31 | convolution fusion | flops 126223904 | bytes 4626432 | tf_op jit(solution)/shard_map/bmn,bmd->bnd/dot_general | solution.py:88
  36.0 2.0 reshape.96
  38.0 2.2 copy.29
  40.2 8.2 %all-to-all-done = bf16[6,16,2,1280]{3,2,0,1:T(2,128)(2,1)} async-done(((bf16[6,16,2,1280]{3,2,0,1:T(2,128)(2,1)}), bf16[6,16,2,1280]{3,2,0,1:T(2,128)(2,1)}, u32[]{:S(2)}, u32[]{:S(2)}) %all-to-all-start) | async-done | bytes 491552 | tf_op jit(solution)/shard_map/all_to_all | solution.py:83
  48.4 4.1 %all-to-all-start.2 = ((bf16[6,16,2,1280]{3,2,0,1:T(2,128)(2,1)}), bf16[6,16,2,1280]{3,2,0,1:T(2,128)(2,1)}, u32[]{:S(2)}, u32[]{:S(2)}) async-start(bf16[6,16,2,1280]{3,2,0,1:T(2,128)(2,1)} %copy.29), calls=%async_computation.2 | async-start | bytes 983040 | tf_op jit(solution)/shard_map/all_to_all | solution.py:92
  52.5 2.0 reshape.93
  54.5 2.0 collective-permute-start
  56.5 11.5 %all-to-all-done.2 = bf16[6,16,2,1280]{3,2,0,1:T(2,128)(2,1)} async-done(((bf16[6,16,2,1280]{3,2,0,1:T(2,128)(2,1)}), bf16[6,16,2,1280]{3,2,0,1:T(2,128)(2,1)}, u32[]{:S(2)}, u32[]{:S(2)}) %all-to-all-start.2) | async-done | bytes 491552 | tf_op jit(solution)/shard_map/all_to_all | solution.py:92
  68.0 2.0 reshape.97
  70.0 2.0 collective-permute-start.2
  75.3 1.4 fusion.22
  76.7 7.4 %collective-permute-done.2 = bf16[192,1280]{1,0:T(8,128)(2,1)S(1)} collective-permute-done((bf16[192,1280]{1,0:T(8,128)(2,1)}, bf16[192,1280]{1,0:T(8,128)(2,1)S(1)}, u32[]{:S(2)}, u32[]{:S(2)}) %collective-permute-start.2) | collective-permute-done | bytes 491552 | tf_op jit(solution)/shard_map/ppermute | solution.py:20
  84.1 2.1 fusion.30
  87.2 3.7 %convolution_convert_fusion = bf16[1280,1280]{1,0:T(8,128)(2,1)} fusion(bf16[384,1280]{1,0:T(8,128)(2,1)S(1)} %constant_dynamic-update-slice_fusion, bf16[384,1280]{1,0:T(8,128)(2,1)S(1)} %fusion.30), kind=kOutput, calls=%fused_computation.18 | convolution fusion | flops 1259929600 | bytes 5242880 | tf_op jit(solution)/shard_map/dot_general | solution.py:47
  91.0 2.8 %fusion.20 = f32[384,1280]{1,0:T(8,128)S(1)} fusion(bf16[384,1280]{1,0:T(8,128)(2,1)} %copy-done.19, bf16[1,1280,1280]{2,1,0:T(8,128)(2,1)S(1)} %copy-done), kind=kOutput, calls=%fused_computation.25 | convolution fusion | flops 1258291200 | bytes 6225920 | tf_op jit(solution)/shard_map/dot_general | solution.py:53
  93.9 2.1 collective-permute-start.3
  96.0 1.8 fusion.18
  100.9 21.8 %collective-permute-done.3 = bf16[192,1280]{1,0:T(8,128)(2,1)S(1)} collective-permute-done((bf16[192,1280]{1,0:T(8,128)(2,1)S(1)}, bf16[192,1280]{1,0:T(8,128)(2,1)S(1)}, u32[]{:S(2)}, u32[]{:S(2)}) %collective-permute-start.3) | collective-permute-done | bytes 491552 | tf_op jit(solution)/shard_map/ppermute | solution.py:20
  123.5 2.0 reshape.98
  125.5 7.6 %all-to-all-start.3 = ((bf16[96,1,2,1280]{3,2,1,0:T(2,128)(2,1)}), bf16[96,1,2,1280]{3,2,1,0:T(2,128)(2,1)}, u32[]{:S(2)}, u32[]{:S(2)}) async-start(bf16[96,1,2,1280]{3,2,1,0:T(2,128)(2,1)} %bitcast.81), calls=%async_computation.3 | async-start | bytes 983040 | tf_op jit(solution)/shard_map/all_to_all | solution.py:103
  133.1 5.7 %convolution_convert_fusion.1 = bf16[1280,1280]{1,0:T(8,128)(2,1)} fusion(bf16[384,1280]{1,0:T(8,128)(2,1)} %copy-done.9, f32[384,1280]{1,0:T(8,128)} %copy-done.17), kind=kOutput, calls=%fused_computation.19 | convolution fusion | flops 1264353280 | bytes 6225920 | tf_op jit(solution)/shard_map/dot_general | solution.py:47
  138.8 15.9 %collective-permute-done.1 = bf16[192,1280]{1,0:T(8,128)(2,1)} collective-permute-done((bf16[192,1280]{1,0:T(8,128)(2,1)}, bf16[192,1280]{1,0:T(8,128)(2,1)}, u32[]{:S(2)}, u32[]{:S(2)}) %collective-permute-start.1) | collective-permute-done | bytes 491552 | tf_op jit(solution)/shard_map/ppermute | solution.py:20
  154.8 2.2 fusion.49
  157.0 2.0 reshape.94
  159.0 8.1 %all-to-all-start.1 = ((bf16[96,1,2,1280]{3,2,1,0:T(2,128)(2,1)}), bf16[96,1,2,1280]{3,2,1,0:T(2,128)(2,1)}, u32[]{:S(2)}, u32[]{:S(2)}) async-start(bf16[96,1,2,1280]{3,2,1,0:T(2,128)(2,1)} %bitcast.82), calls=%async_computation.1 | async-start | bytes 983040 | tf_op jit(solution)/shard_map/all_to_all | solution.py:103
  167.8 2.1 copy.31
  169.9 2.0 reshape.99
  171.9 11.7 %all-to-all-done.1 = bf16[96,1,2,1280]{3,2,1,0:T(2,128)(2,1)} async-done(((bf16[96,1,2,1280]{3,2,1,0:T(2,128)(2,1)}), bf16[96,1,2,1280]{3,2,1,0:T(2,128)(2,1)}, u32[]{:S(2)}, u32[]{:S(2)}) %all-to-all-start.1) | async-done | bytes 491552 | tf_op jit(solution)/shard_map/all_to_all | solution.py:103
  183.6 2.2 copy.28
  185.7 2.0 reshape.95
  187.7 3.6 %convolution_bitcast_fusion.1 = f32[6,256,32]{1,2,0:T(8,128)S(1)} fusion(bf16[6,32,1280]{2,1,0:T(8,128)(2,1)} %reshape.95, bf16[6,256,1280]{2,1,0:T(8,128)(2,1)} %param.7), kind=kOutput, calls=%fused_computation.55 | convolution fusion | flops 125829120 | bytes 4620288 | tf_op jit(solution)/shard_map/bmd,bnd->bmn/dot_general | solution.py:121
  191.8 1.5 fusion.69
  194.2 1.6 convolution_bitcast_fusion
  198.8 1.5 maximum_maximum_fusion
  200.3 3.4 %all-to-all-start.4 = ((f32[16,24,128]{2,1,0:T(8,128)}), f32[16,24,128]{2,1,0:T(8,128)S(1)}, u32[]{:S(2)}, u32[]{:S(2)}) async-start(f32[16,24,128]{2,1,0:T(8,128)} %bitcast.84), calls=%async_computation.4 | async-start | bytes 393216 | tf_op jit(solution)/shard_map/all_to_all | solution.py:69
  204.7 7.8 %multiply_reduce_fusion = (f32[6,256]{1,0:T(8,128)S(1)}, f32[6,256]{1,0:T(8,128)S(1)}, f32[6,256,1280]{2,1,0:T(8,128)}) fusion(f32[1280]{0:T(1024)} %param.8, f32[6,256]{1,0:T(8,128)S(1)} %add_rsqrt_fusion, f32[6,256]{1,0:T(8,128)S(1)} %broadcast_multiply_fusion.2, bf16[6,256,1280]{2,1,0:T(8,128)(2,1)} %param.6, ...), kind=kOutput, calls=%fused_computation.20 | convolution fusion | flops 396555264 | bytes 13104128 | tf_op jit(solution)/shard_map/bmn,bnd->bmd/dot_general | solution.py:145
  214.3 9.5 %all-to-all-start.5 = ((f32[16,24,128]{2,1,0:T(8,128)}), f32[16,24,128]{2,1,0:T(8,128)S(1)}, u32[]{:S(2)}, u32[]{:S(2)}) async-start(f32[16,24,128]{2,1,0:T(8,128)} %broadcast_in_dim.14), calls=%async_computation.5 | async-start | bytes 393216 | tf_op jit(solution)/shard_map/all_to_all | solution.py:14
  224.5 7.5 %all-to-all-done.5 = f32[16,24,128]{2,1,0:T(8,128)S(1)} async-done(((f32[16,24,128]{2,1,0:T(8,128)}), f32[16,24,128]{2,1,0:T(8,128)S(1)}, u32[]{:S(2)}, u32[]{:S(2)}) %all-to-all-start.5) | async-done | bytes 196640 | tf_op jit(solution)/shard_map/all_to_all | solution.py:14
  232.7 5.7 %all-to-all-start.6 = ((f32[16,24,128]{2,1,0:T(8,128)}), f32[16,24,128]{2,1,0:T(8,128)S(1)}, u32[]{:S(2)}, u32[]{:S(2)}) async-start(f32[16,24,128]{2,1,0:T(8,128)} %broadcast_in_dim.15), calls=%async_computation.6 | async-start | bytes 393216 | tf_op jit(solution)/shard_map/all_to_all | solution.py:14
  238.4 8.5 %fusion.14 = bf16[6,256,1280]{2,1,0:T(8,128)(2,1)} fusion(bf16[6,256,1280]{2,1,0:T(8,128)(2,1)} %param.6, bf16[6,256,1280]{2,1,0:T(8,128)(2,1)} %param.7, f32[6,256,1280]{2,1,0:T(8,128)} %get-tuple-element.19, f32[6,256]{1,0:T(8,128)} %get-tuple-element.20, f32[6,256]{1,0:T(8,128)} %get-tuple-element.21, f32[1280]{0:T(1024)} %param.8, ...), kind=kLoop, calls=%fused_computation.16 | loop fusion | flops 21626880 | bytes 19690496 | tf_op jit(solution)/shard_map/convert_element_type | solution.py:150
  246.9 1.7 all-to-all-done.6
  250.6 8.5 %reduce-scatter.5.cloned.1.call-done = bf16[160,1280]{1,0:T(8,128)(2,1)} async-done(((bf16[1280,1280]{1,0:T(8,128)(2,1)}), bf16[160,1280]{1,0:T(8,128)(2,1)}) %reduce-scatter.5.cloned.1.call-update) | async-done | bytes 409616 | tf_op jit(solution)/shard_map/reduce_scatter | solution.py:115
  (83 shorter events, 24.3 us)
Async XLA Ops:
  7.2 68.1 %copy-start = (bf16[1,1280,1280]{2,1,0:T(8,128)(2,1)S(1)}, bf16[1,1280,1280]{2,1,0:T(8,128)(2,1)}, u32[]{:S(2)}) copy-start(bf16[1,1280,1280]{2,1,0:T(8,128)(2,1)} %param.10) | copy-start | bytes 9830404
  7.2 3.4 %copy-start.1 = (bf16[6,256,1280]{2,1,0:T(8,128)(2,1)S(1)}, bf16[6,256,1280]{2,1,0:T(8,128)(2,1)}, u32[]{:S(2)}) copy-start(bf16[6,256,1280]{2,1,0:T(8,128)(2,1)} %param.6) | copy-start | bytes 11796484
  7.2 4.6 %copy-start.14 = (f32[1280]{0:T(1024)S(1)}, f32[1280]{0:T(1024)}, u32[]{:S(2)}) copy-start(f32[1280]{0:T(1024)} %param.8) | copy-start | bytes 15364
  7.2 4.6 %copy-start.7 = (bf16[1280,32]{0,1:T(8,128)(2,1)S(1)}, bf16[1280,32]{0,1:T(8,128)(2,1)}, u32[]{:S(2)}) copy-start(bf16[1280,32]{0,1:T(8,128)(2,1)} %param.9) | copy-start | bytes 245764
  10.6 194.0 %copy-start.12 = (f32[6,256]{1,0:T(8,128)}, f32[6,256]{1,0:T(8,128)S(1)}, u32[]{:S(2)}) copy-start(f32[6,256]{1,0:T(8,128)S(1)} %broadcast_multiply_fusion.2) | copy-start | bytes 18436
  11.8 192.8 %copy-start.13 = (f32[6,256]{1,0:T(8,128)}, f32[6,256]{1,0:T(8,128)S(1)}, u32[]{:S(2)}) copy-start(f32[6,256]{1,0:T(8,128)S(1)} %add_rsqrt_fusion) | copy-start | bytes 18436
  14.6 0.7 copy-start.5
  15.4 0.6 copy-start.11
  22.6 25.8 %all-to-all-start = ((bf16[6,16,2,1280]{3,2,0,1:T(2,128)(2,1)}), bf16[6,16,2,1280]{3,2,0,1:T(2,128)(2,1)}, u32[]{:S(2)}, u32[]{:S(2)}) async-start(bf16[6,16,2,1280]{3,2,0,1:T(2,128)(2,1)} %copy.26), calls=%async_computation | async-start | bytes 983040 | tf_op jit(solution)/shard_map/all_to_all | solution.py:83
  48.4 19.7 %all-to-all-start.2 = ((bf16[6,16,2,1280]{3,2,0,1:T(2,128)(2,1)}), bf16[6,16,2,1280]{3,2,0,1:T(2,128)(2,1)}, u32[]{:S(2)}, u32[]{:S(2)}) async-start(bf16[6,16,2,1280]{3,2,0,1:T(2,128)(2,1)} %copy.29), calls=%async_computation.2 | async-start | bytes 983040 | tf_op jit(solution)/shard_map/all_to_all | solution.py:92
  52.5 198.1 %reduce-scatter.3.cloned.1.call-start = ((), (), s32[]{:S(2)}) async-start(), calls=%async_computation.9 | async-start | bytes 3686400 | tf_op jit(solution)/shard_map/reduce_scatter | solution.py:116
  54.5 19.6 %collective-permute-start = (bf16[192,1280]{1,0:T(8,128)(2,1)}, bf16[192,1280]{1,0:T(8,128)(2,1)}, u32[]{:S(2)}, u32[]{:S(2)}) collective-permute-start(bf16[192,1280]{1,0:T(8,128)(2,1)} %reshape.93), channel_id=1, source_target_pairs={{0,1},{1,0},{2,3},{3,2},{4,5},{5,4},{6,7},{7,6},{8,9},{9,8},{10,11... | collective-permute-start | bytes 1474568 | tf_op jit(solution)/shard_map/ppermute | solution.py:20
  70.0 14.1 %collective-permute-start.2 = (bf16[192,1280]{1,0:T(8,128)(2,1)}, bf16[192,1280]{1,0:T(8,128)(2,1)S(1)}, u32[]{:S(2)}, u32[]{:S(2)}) collective-permute-start(bf16[192,1280]{1,0:T(8,128)(2,1)} %reshape.97), channel_id=1, source_target_pairs={{0,1},{1,0},{2,3},{3,2},{4,5},{5,4},{6,7},{7,6},{8,9},{9,8},{10,11... | collective-permute-start | bytes 1474568 | tf_op jit(solution)/shard_map/ppermute | solution.py:20
  75.3 8.9 %copy-start.15 = (bf16[1,1280,1280]{2,1,0:T(8,128)(2,1)S(1)}, bf16[1,1280,1280]{2,1,0:T(8,128)(2,1)}, u32[]{:S(2)}) copy-start(bf16[1,1280,1280]{2,1,0:T(8,128)(2,1)} %param.11) | copy-start | bytes 9830404
  76.7 9.5 %copy-start.17 = (f32[384,1280]{1,0:T(8,128)}, f32[384,1280]{1,0:T(8,128)S(1)}, u32[]{:S(2)}) copy-start(f32[384,1280]{1,0:T(8,128)S(1)} %fusion.22) | copy-start | bytes 5898244
  84.1 2.1 copy-start.9
  86.3 1.0 copy-start.19
  91.0 5.0 %copy-start.16 = (bf16[1,1280,1280]{2,1,0:T(8,128)(2,1)S(1)}, bf16[1,1280,1280]{2,1,0:T(8,128)(2,1)}, u32[]{:S(2)}) copy-start(bf16[1,1280,1280]{2,1,0:T(8,128)(2,1)} %param.11) | copy-start | bytes 9830404
  91.0 5.0 %copy-start.18 = (f32[384,1280]{1,0:T(8,128)S(1)}, f32[384,1280]{1,0:T(8,128)}, u32[]{:S(2)}) copy-start(f32[384,1280]{1,0:T(8,128)} %copy-done.17) | copy-start | bytes 5898244
  93.9 28.7 %collective-permute-start.3 = (bf16[192,1280]{1,0:T(8,128)(2,1)S(1)}, bf16[192,1280]{1,0:T(8,128)(2,1)S(1)}, u32[]{:S(2)}, u32[]{:S(2)}) collective-permute-start(bf16[192,1280]{1,0:T(8,128)(2,1)S(1)} %slice.59), channel_id=1, source_target_pairs={{0,1},{1,0},{2,3},{3,2},{4,5},{5,4},{6,7},{7,6},{8,9},{9,8},{10,11... | collective-permute-start | bytes 1474568 | tf_op jit(solution)/shard_map/ppermute | solution.py:20
  97.8 1.3 copy-start.4
  99.9 54.9 %collective-permute-start.1 = (bf16[192,1280]{1,0:T(8,128)(2,1)}, bf16[192,1280]{1,0:T(8,128)(2,1)}, u32[]{:S(2)}, u32[]{:S(2)}) collective-permute-start(bf16[192,1280]{1,0:T(8,128)(2,1)} %slice.60), channel_id=1, source_target_pairs={{0,1},{1,0},{2,3},{3,2},{4,5},{5,4},{6,7},{7,6},{8,9},{9,8},{10,11... | collective-permute-start | bytes 1474568 | tf_op jit(solution)/shard_map/ppermute | solution.py:20
  125.5 33.5 %all-to-all-start.3 = ((bf16[96,1,2,1280]{3,2,1,0:T(2,128)(2,1)}), bf16[96,1,2,1280]{3,2,1,0:T(2,128)(2,1)}, u32[]{:S(2)}, u32[]{:S(2)}) async-start(bf16[96,1,2,1280]{3,2,1,0:T(2,128)(2,1)} %bitcast.81), calls=%async_computation.3 | async-start | bytes 983040 | tf_op jit(solution)/shard_map/all_to_all | solution.py:103
  133.1 126.0 %reduce-scatter.5.cloned.1.call-start = ((), (), s32[]{:S(2)}) async-start(), calls=%async_computation.10 | async-start | bytes 3686400 | tf_op jit(solution)/shard_map/reduce_scatter | solution.py:115
  159.0 24.6 %all-to-all-start.1 = ((bf16[96,1,2,1280]{3,2,1,0:T(2,128)(2,1)}), bf16[96,1,2,1280]{3,2,1,0:T(2,128)(2,1)}, u32[]{:S(2)}, u32[]{:S(2)}) async-start(bf16[96,1,2,1280]{3,2,1,0:T(2,128)(2,1)} %bitcast.82), calls=%async_computation.1 | async-start | bytes 983040 | tf_op jit(solution)/shard_map/all_to_all | solution.py:103
  183.6 7.8 %copy-start.10 = (f32[6,256,32]{1,2,0:T(8,128)S(1)}, f32[6,256,32]{1,2,0:T(8,128)}, u32[]{:S(2)}) copy-start(f32[6,256,32]{1,2,0:T(8,128)} %get-tuple-element.18) | copy-start | bytes 589828
  187.7 4.0 %copy-start.2 = (bf16[6,256,1280]{2,1,0:T(8,128)(2,1)S(1)}, bf16[6,256,1280]{2,1,0:T(8,128)(2,1)}, u32[]{:S(2)}) copy-start(bf16[6,256,1280]{2,1,0:T(8,128)(2,1)} %param.6) | copy-start | bytes 11796484
  187.7 4.0 %copy-start.3 = (bf16[6,32,1280]{2,1,0:T(8,128)(2,1)S(1)}, bf16[6,32,1280]{2,1,0:T(8,128)(2,1)}, u32[]{:S(2)}) copy-start(bf16[6,32,1280]{2,1,0:T(8,128)(2,1)} %reshape.99) | copy-start | bytes 1474564
  191.8 1.5 copy-start.6
  194.2 1.6 copy-start.20
  194.2 1.6 copy-start.21
  200.3 13.3 %all-to-all-start.4 = ((f32[16,24,128]{2,1,0:T(8,128)}), f32[16,24,128]{2,1,0:T(8,128)S(1)}, u32[]{:S(2)}, u32[]{:S(2)}) async-start(f32[16,24,128]{2,1,0:T(8,128)} %bitcast.84), calls=%async_computation.4 | async-start | bytes 393216 | tf_op jit(solution)/shard_map/all_to_all | solution.py:69
  214.3 17.6 %all-to-all-start.5 = ((f32[16,24,128]{2,1,0:T(8,128)}), f32[16,24,128]{2,1,0:T(8,128)S(1)}, u32[]{:S(2)}, u32[]{:S(2)}) async-start(f32[16,24,128]{2,1,0:T(8,128)} %broadcast_in_dim.14), calls=%async_computation.5 | async-start | bytes 393216 | tf_op jit(solution)/shard_map/all_to_all | solution.py:14
  232.7 15.9 %all-to-all-start.6 = ((f32[16,24,128]{2,1,0:T(8,128)}), f32[16,24,128]{2,1,0:T(8,128)S(1)}, u32[]{:S(2)}, u32[]{:S(2)}) async-start(f32[16,24,128]{2,1,0:T(8,128)} %broadcast_in_dim.15), calls=%async_computation.6 | async-start | bytes 393216 | tf_op jit(solution)/shard_map/all_to_all | solution.py:14
  238.4 10.2 %copy-start.8 = (bf16[1280,32]{0,1:T(8,128)(2,1)S(1)}, bf16[1280,32]{0,1:T(8,128)(2,1)}, u32[]{:S(2)}) copy-start(bf16[1280,32]{0,1:T(8,128)(2,1)} %param.9) | copy-start | bytes 245764
Sparse Core Ops, SparseCore 0:
  91.1 90.7 reduce-scatter.2
  185.0 74.0 reduce-scatter.4
where the time goes:
time: 268 us; the launch traced here: 266 us
  waiting for transfers between devices  95.2 us (36%)
  starting transfers between devices  54.8 us (20%)
  matrix products  39.8 us (15%)
  local copies, waits for them, and re-layouts  36.9 us (14%)
  other arithmetic  24.8 us (9%)
  between operations  14.5 us (5%)
    ppermute x4, waiting for transfers between devices, swapped(): return lax.ppermute(value, 'tensor', [(0, 1), (1, 0)])  45.1 us
    all_to_all x2, starting transfers between devices, reduced_and_returned(): lax.all_to_all(total.reshape(arrived.shape), 'expert', split_axis=0, conc...  15.7 us
    all_to_all x2, starting transfers between devices, from_everyone(): lax.all_to_all(jnp.broadcast_to(shard[None], (devices, *shard.shape)), ax...  15.2 us
    all_to_all x2, waiting for transfers between devices, reduced_and_returned(): lax.all_to_all(total.reshape(arrived.shape), 'expert', split_axis=0, conc...  11.7 us
    all_to_all x1, waiting for transfers between devices, local(): lax.all_to_all(grad_slots, 'expert', split_axis=1, concat_axis=0, tiled=T...  11.5 us
    dot_general x2, matrix products, contract_rows(): lax.dot_general(left, right, (((0,), (0,)), ((), ())), preferred_element_...  9.39 us
    all_to_all x2, waiting for transfers between devices, from_everyone(): lax.all_to_all(jnp.broadcast_to(shard[None], (devices, *shard.shape)), ax...  9.2 us
    all_to_all x1, starting transfers between devices, local(): lax.all_to_all(slot_inputs, 'expert', split_axis=1, concat_axis=0, tiled=...  9.15 us
  transfers between devices with their start and end apart: 13, of which 10 were waited for; matrix products, arithmetic and copies ran while one was open for 29% of the time, Pallas kernels for 0%

commit v1 on v0

--- a/solution.py
+++ b/solution.py
@@ -80,7 +80,10 @@
     slot_values, combine, saved = mixing_forward(tokens, norm_gain, slot_keys)
     slot_low = slot_values.astype(jnp.bfloat16)
     slot_inputs = slot_low.reshape(local_imgs, experts, SLOT_PER, features)
-    arrived = lax.all_to_all(slot_inputs, "expert", split_axis=1, concat_axis=0, tiled=True)
+    size = lax.axis_size("expert")
+    parts = jnp.stack(jnp.split(slot_inputs, size, axis=1), axis=0)
+    parts = lax.all_to_all(parts, "expert", split_axis=0, concat_axis=0)
+    arrived = jnp.concatenate(parts, axis=0)
     own = arrived.reshape(-1, features)
     half = own.shape[0]
     slot_rows = jnp.concatenate([own, swapped(own)])

time: 268 us -> 289 us (1.078)
  local copies, waits for them, and re-layouts: 36.9 us -> 56.9 us
    unnamed x46 -> x61, local copies, waits for them, and re-layouts: 6.33 us -> 27.1 us
    another operation x0 -> x2, local copies, waits for them, and re-layouts: none -> 3.38 us  [the longest x1 1.99 us: local(): own = arrived.reshape(-1, features)]
  transfers between devices with their start and end apart: 13 -> 13, of which waited for: 10 -> 10; matrix products, arithmetic and copies ran while one was open for 29% -> 27% of each run, Pallas kernels for 0% -> 0%
where the time goes in v1:
time: 289 us; the launch traced here: 286 us
  waiting for transfers between devices  95.2 us (33%)
  local copies, waits for them, and re-layouts  56.9 us (20%)
  starting transfers between devices  54.8 us (19%)
  matrix products  39.8 us (14%)
  other arithmetic  24.8 us (9%)
  between operations  14.5 us (5%)
    ppermute x4, waiting for transfers between devices, swapped(): return lax.ppermute(value, 'tensor', [(0, 1), (1, 0)])  45.1 us
    unnamed x61, local copies, waits for them, and re-layouts  27.1 us
    all_to_all x2, starting transfers between devices, reduced_and_returned(): lax.all_to_all(total.reshape(arrived.shape), 'expert', split_axis=0, conc...  15.7 us
    all_to_all x2, starting transfers between devices, from_everyone(): lax.all_to_all(jnp.broadcast_to(shard[None], (devices, *shard.shape)), ax...  15.2 us
    all_to_all x2, waiting for transfers between devices, reduced_and_returned(): lax.all_to_all(total.reshape(arrived.shape), 'expert', split_axis=0, conc...  11.7 us
    all_to_all x1, waiting for transfers between devices, local(): lax.all_to_all(grad_slots, 'expert', split_axis=1, concat_axis=0, tiled=T...  11.5 us
    dot_general x2, matrix products, contract_rows(): lax.dot_general(left, right, (((0,), (0,)), ((), ())), preferred_element_...  9.39 us
    all_to_all x2, waiting for transfers between devices, from_everyone(): lax.all_to_all(jnp.broadcast_to(shard[None], (devices, *shard.shape)), ax...  9.2 us
  transfers between devices with their start and end apart: 13, of which 10 were waited for; matrix products, arithmetic and copies ran while one was open for 27% of the time, Pallas kernels for 0%

profile of v1, /device:TPU:11, one launch (start us, length us, event | category | flops | bytes accessed | tf_op | source)
XLA Modules:
  0.0 285.9 jit_solution(12586751814353058134)
XLA Ops:
  7.2 2.8 convert_reduce_fusion
  11.8 1.7 fusion.61
  16.0 2.4 convolution_convert_fusion.3
  18.4 2.0 reshape.88
  37.0 1.4 constant_dynamic-update-slice_fusion.3
  42.5 9.2 %all-to-all-start = ((bf16[16,6,1,2,1280]{4,3,1,2,0:T(2,128)(2,1)}), bf16[16,6,1,2,1280]{4,3,1,2,0:T(2,128)(2,1)}, u32[]{:S(2)}, u32[]{:S(2)}) async-start(bf16[16,6,1,2,1280]{4,3,1,2,0:T(2,128)(2,1)} %constant_dynamic-update-slice_fusion), calls=%async_computation | async-start | bytes 983040 | tf_op jit(solution)/shard_map/all_to_all | solution.py:85
  52.4 3.6 %convolution_convert_fusion.2 = bf16[6,32,1280]{2,1,0:T(8,128)(2,1)} fusion(bf16[6,256,1280]{2,1,0:T(8,128)(2,1)} %param.7, f32[6,256]{1,0:T(8,128)S(1)} %get-tuple-element.17, f32[6,256,32]{1,2,0:T(8,128)S(1)} %fusion.61), kind=kOutput, calls=%fused_computation.31 | convolution fusion | flops 126223904 | bytes 4626432 | tf_op jit(solution)/shard_map/bmn,bmd->bnd/dot_general | solution.py:91
  56.0 2.0 reshape.91
  58.0 2.2 copy.86
  60.2 8.2 %all-to-all-done = bf16[16,6,1,2,1280]{4,3,1,2,0:T(2,128)(2,1)} async-done(((bf16[16,6,1,2,1280]{4,3,1,2,0:T(2,128)(2,1)}), bf16[16,6,1,2,1280]{4,3,1,2,0:T(2,128)(2,1)}, u32[]{:S(2)}, u32[]{:S(2)}) %all-to-all-start) | async-done | bytes 491552 | tf_op jit(solution)/shard_map/all_to_all | solution.py:85
  68.3 4.1 %all-to-all-start.2 = ((bf16[6,16,2,1280]{3,2,0,1:T(2,128)(2,1)}), bf16[6,16,2,1280]{3,2,0,1:T(2,128)(2,1)}, u32[]{:S(2)}, u32[]{:S(2)}) async-start(bf16[6,16,2,1280]{3,2,0,1:T(2,128)(2,1)} %copy.86), calls=%async_computation.2 | async-start | bytes 983040 | tf_op jit(solution)/shard_map/all_to_all | solution.py:95
  72.5 2.0 reshape_reshape.3
  74.5 2.0 collective-permute-start
  76.5 11.5 %all-to-all-done.2 = bf16[6,16,2,1280]{3,2,0,1:T(2,128)(2,1)} async-done(((bf16[6,16,2,1280]{3,2,0,1:T(2,128)(2,1)}), bf16[6,16,2,1280]{3,2,0,1:T(2,128)(2,1)}, u32[]{:S(2)}, u32[]{:S(2)}) %all-to-all-start.2) | async-done | bytes 491552 | tf_op jit(solution)/shard_map/all_to_all | solution.py:95
  88.0 2.0 reshape.92
  90.0 2.0 collective-permute-start.2
  95.2 1.4 fusion.22
  96.7 7.4 %collective-permute-done.2 = bf16[192,1280]{1,0:T(8,128)(2,1)S(1)} collective-permute-done((bf16[192,1280]{1,0:T(8,128)(2,1)}, bf16[192,1280]{1,0:T(8,128)(2,1)S(1)}, u32[]{:S(2)}, u32[]{:S(2)}) %collective-permute-start.2) | collective-permute-done | bytes 491552 | tf_op jit(solution)/shard_map/ppermute | solution.py:20
  104.1 2.1 fusion.30
  107.2 3.7 %convolution_convert_fusion = bf16[1280,1280]{1,0:T(8,128)(2,1)} fusion(bf16[384,1280]{1,0:T(8,128)(2,1)S(1)} %constant_dynamic-update-slice_fusion.16, bf16[384,1280]{1,0:T(8,128)(2,1)S(1)} %fusion.30), kind=kOutput, calls=%fused_computation.18 | convolution fusion | flops 1259929600 | bytes 5242880 | tf_op jit(solution)/shard_map/dot_general | solution.py:47
  111.0 2.8 fusion.20
  113.8 2.1 collective-permute-start.3
  116.0 1.8 fusion.18
  120.8 21.8 %collective-permute-done.3 = bf16[192,1280]{1,0:T(8,128)(2,1)S(1)} collective-permute-done((bf16[192,1280]{1,0:T(8,128)(2,1)S(1)}, bf16[192,1280]{1,0:T(8,128)(2,1)S(1)}, u32[]{:S(2)}, u32[]{:S(2)}) %collective-permute-start.3) | collective-permute-done | bytes 491552 | tf_op jit(solution)/shard_map/ppermute | solution.py:20
  143.5 2.0 reshape.93
  145.5 7.6 %all-to-all-start.3 = ((bf16[96,1,2,1280]{3,2,1,0:T(2,128)(2,1)}), bf16[96,1,2,1280]{3,2,1,0:T(2,128)(2,1)}, u32[]{:S(2)}, u32[]{:S(2)}) async-start(bf16[96,1,2,1280]{3,2,1,0:T(2,128)(2,1)} %bitcast.172), calls=%async_computation.3 | async-start | bytes 983040 | tf_op jit(solution)/shard_map/all_to_all | solution.py:106
  153.1 5.7 %convolution_convert_fusion.1 = bf16[1280,1280]{1,0:T(8,128)(2,1)} fusion(bf16[384,1280]{1,0:T(8,128)(2,1)} %copy-done.9, f32[384,1280]{1,0:T(8,128)} %copy-done.17), kind=kOutput, calls=%fused_computation.19 | convolution fusion | flops 1264353280 | bytes 6225920 | tf_op jit(solution)/shard_map/dot_general | solution.py:47
  158.8 15.9 %collective-permute-done.1 = bf16[192,1280]{1,0:T(8,128)(2,1)} collective-permute-done((bf16[192,1280]{1,0:T(8,128)(2,1)}, bf16[192,1280]{1,0:T(8,128)(2,1)}, u32[]{:S(2)}, u32[]{:S(2)}) %collective-permute-start.1) | collective-permute-done | bytes 491552 | tf_op jit(solution)/shard_map/ppermute | solution.py:20
  174.7 2.2 fusion.49
  176.9 2.0 reshape.89
  178.9 8.1 %all-to-all-start.1 = ((bf16[96,1,2,1280]{3,2,1,0:T(2,128)(2,1)}), bf16[96,1,2,1280]{3,2,1,0:T(2,128)(2,1)}, u32[]{:S(2)}, u32[]{:S(2)}) async-start(bf16[96,1,2,1280]{3,2,1,0:T(2,128)(2,1)} %bitcast.173), calls=%async_computation.1 | async-start | bytes 983040 | tf_op jit(solution)/shard_map/all_to_all | solution.py:106
  187.7 2.1 copy.88
  189.9 2.0 reshape.94
  191.8 11.7 %all-to-all-done.1 = bf16[96,1,2,1280]{3,2,1,0:T(2,128)(2,1)} async-done(((bf16[96,1,2,1280]{3,2,1,0:T(2,128)(2,1)}), bf16[96,1,2,1280]{3,2,1,0:T(2,128)(2,1)}, u32[]{:S(2)}, u32[]{:S(2)}) %all-to-all-start.1) | async-done | bytes 491552 | tf_op jit(solution)/shard_map/all_to_all | solution.py:106
  203.5 2.2 copy.85
  205.7 2.0 reshape.90
  207.7 3.6 %convolution_bitcast_fusion.1 = f32[6,256,32]{1,2,0:T(8,128)S(1)} fusion(bf16[6,32,1280]{2,1,0:T(8,128)(2,1)} %reshape.90, bf16[6,256,1280]{2,1,0:T(8,128)(2,1)} %param.7), kind=kOutput, calls=%fused_computation.55 | convolution fusion | flops 125829120 | bytes 4620288 | tf_op jit(solution)/shard_map/bmd,bnd->bmn/dot_general | solution.py:124
  211.7 1.5 fusion.69
  214.2 1.6 convolution_bitcast_fusion
  218.8 1.5 maximum_maximum_fusion
  220.3 3.4 %all-to-all-start.4 = ((f32[16,24,128]{2,1,0:T(8,128)}), f32[16,24,128]{2,1,0:T(8,128)S(1)}, u32[]{:S(2)}, u32[]{:S(2)}) async-start(f32[16,24,128]{2,1,0:T(8,128)} %bitcast.175), calls=%async_computation.4 | async-start | bytes 393216 | tf_op jit(solution)/shard_map/all_to_all | solution.py:69
  224.6 7.8 %multiply_reduce_fusion = (f32[6,256]{1,0:T(8,128)S(1)}, f32[6,256]{1,0:T(8,128)S(1)}, f32[6,256,1280]{2,1,0:T(8,128)}) fusion(f32[1280]{0:T(1024)} %param.8, f32[6,256]{1,0:T(8,128)S(1)} %add_rsqrt_fusion, f32[6,256]{1,0:T(8,128)S(1)} %broadcast_multiply_fusion.2, bf16[6,256,1280]{2,1,0:T(8,128)(2,1)} %param.6, ...), kind=kOutput, calls=%fused_computation.20 | convolution fusion | flops 396555264 | bytes 13104128 | tf_op jit(solution)/shard_map/bmn,bnd->bmd/dot_general | solution.py:148
  234.3 9.5 %all-to-all-start.5 = ((f32[16,24,128]{2,1,0:T(8,128)}), f32[16,24,128]{2,1,0:T(8,128)S(1)}, u32[]{:S(2)}, u32[]{:S(2)}) async-start(f32[16,24,128]{2,1,0:T(8,128)} %broadcast_in_dim.14), calls=%async_computation.5 | async-start | bytes 393216 | tf_op jit(solution)/shard_map/all_to_all | solution.py:14
  244.4 7.5 %all-to-all-done.5 = f32[16,24,128]{2,1,0:T(8,128)S(1)} async-done(((f32[16,24,128]{2,1,0:T(8,128)}), f32[16,24,128]{2,1,0:T(8,128)S(1)}, u32[]{:S(2)}, u32[]{:S(2)}) %all-to-all-start.5) | async-done | bytes 196640 | tf_op jit(solution)/shard_map/all_to_all | solution.py:14
  252.7 5.7 %all-to-all-start.6 = ((f32[16,24,128]{2,1,0:T(8,128)}), f32[16,24,128]{2,1,0:T(8,128)S(1)}, u32[]{:S(2)}, u32[]{:S(2)}) async-start(f32[16,24,128]{2,1,0:T(8,128)} %broadcast_in_dim.15), calls=%async_computation.6 | async-start | bytes 393216 | tf_op jit(solution)/shard_map/all_to_all | solution.py:14
  258.4 8.5 %fusion.14 = bf16[6,256,1280]{2,1,0:T(8,128)(2,1)} fusion(bf16[6,256,1280]{2,1,0:T(8,128)(2,1)} %param.6, bf16[6,256,1280]{2,1,0:T(8,128)(2,1)} %param.7, f32[6,256,1280]{2,1,0:T(8,128)} %get-tuple-element.19, f32[6,256]{1,0:T(8,128)} %get-tuple-element.20, f32[6,256]{1,0:T(8,128)} %get-tuple-element.21, f32[1280]{0:T(1024)} %param.8, ...), kind=kLoop, calls=%fused_computation.16 | loop fusion | flops 21626880 | bytes 19690496 | tf_op jit(solution)/shard_map/convert_element_type | solution.py:153
  266.8 1.7 all-to-all-done.6
  270.6 8.5 %reduce-scatter.5.cloned.1.call-done = bf16[160,1280]{1,0:T(8,128)(2,1)} async-done(((bf16[1280,1280]{1,0:T(8,128)(2,1)}), bf16[160,1280]{1,0:T(8,128)(2,1)}) %reduce-scatter.5.cloned.1.call-update) | async-done | bytes 409616 | tf_op jit(solution)/shard_map/reduce_scatter | solution.py:118
  (98 shorter events, 45.0 us)
Async XLA Ops:
  7.2 88.0 %copy-start = (bf16[1,1280,1280]{2,1,0:T(8,128)(2,1)S(1)}, bf16[1,1280,1280]{2,1,0:T(8,128)(2,1)}, u32[]{:S(2)}) copy-start(bf16[1,1280,1280]{2,1,0:T(8,128)(2,1)} %param.10) | copy-start | bytes 9830404
  7.2 3.4 %copy-start.1 = (bf16[6,256,1280]{2,1,0:T(8,128)(2,1)S(1)}, bf16[6,256,1280]{2,1,0:T(8,128)(2,1)}, u32[]{:S(2)}) copy-start(bf16[6,256,1280]{2,1,0:T(8,128)(2,1)} %param.6) | copy-start | bytes 11796484
  7.2 4.6 %copy-start.14 = (f32[1280]{0:T(1024)S(1)}, f32[1280]{0:T(1024)}, u32[]{:S(2)}) copy-start(f32[1280]{0:T(1024)} %param.8) | copy-start | bytes 15364
  7.2 4.6 %copy-start.7 = (bf16[1280,32]{0,1:T(8,128)(2,1)S(1)}, bf16[1280,32]{0,1:T(8,128)(2,1)}, u32[]{:S(2)}) copy-start(bf16[1280,32]{0,1:T(8,128)(2,1)} %param.9) | copy-start | bytes 245764
  10.6 214.0 %copy-start.12 = (f32[6,256]{1,0:T(8,128)}, f32[6,256]{1,0:T(8,128)S(1)}, u32[]{:S(2)}) copy-start(f32[6,256]{1,0:T(8,128)S(1)} %broadcast_multiply_fusion.2) | copy-start | bytes 18436
  11.8 212.8 %copy-start.13 = (f32[6,256]{1,0:T(8,128)}, f32[6,256]{1,0:T(8,128)S(1)}, u32[]{:S(2)}) copy-start(f32[6,256]{1,0:T(8,128)S(1)} %add_rsqrt_fusion) | copy-start | bytes 18436
  14.6 0.7 copy-start.5
  15.4 0.6 copy-start.11
  42.5 25.8 %all-to-all-start = ((bf16[16,6,1,2,1280]{4,3,1,2,0:T(2,128)(2,1)}), bf16[16,6,1,2,1280]{4,3,1,2,0:T(2,128)(2,1)}, u32[]{:S(2)}, u32[]{:S(2)}) async-start(bf16[16,6,1,2,1280]{4,3,1,2,0:T(2,128)(2,1)} %constant_dynamic-update-slice_fusion), calls=%async_computation | async-start | bytes 983040 | tf_op jit(solution)/shard_map/all_to_all | solution.py:85
  68.3 19.7 %all-to-all-start.2 = ((bf16[6,16,2,1280]{3,2,0,1:T(2,128)(2,1)}), bf16[6,16,2,1280]{3,2,0,1:T(2,128)(2,1)}, u32[]{:S(2)}, u32[]{:S(2)}) async-start(bf16[6,16,2,1280]{3,2,0,1:T(2,128)(2,1)} %copy.86), calls=%async_computation.2 | async-start | bytes 983040 | tf_op jit(solution)/shard_map/all_to_all | solution.py:95
  72.4 198.1 %reduce-scatter.3.cloned.1.call-start = ((), (), s32[]{:S(2)}) async-start(), calls=%async_computation.9 | async-start | bytes 3686400 | tf_op jit(solution)/shard_map/reduce_scatter | solution.py:119
  74.5 19.6 %collective-permute-start = (bf16[192,1280]{1,0:T(8,128)(2,1)}, bf16[192,1280]{1,0:T(8,128)(2,1)}, u32[]{:S(2)}, u32[]{:S(2)}) collective-permute-start(bf16[192,1280]{1,0:T(8,128)(2,1)} %reshape_reshape.3), channel_id=1, source_target_pairs={{0,1},{1,0},{2,3},{3,2},{4,5},{5,4},{6,7},{7,6},{8,9},{9,8},{10,11... | collective-permute-start | bytes 1474568 | tf_op jit(solution)/shard_map/ppermute | solution.py:20
  90.0 14.1 %collective-permute-start.2 = (bf16[192,1280]{1,0:T(8,128)(2,1)}, bf16[192,1280]{1,0:T(8,128)(2,1)S(1)}, u32[]{:S(2)}, u32[]{:S(2)}) collective-permute-start(bf16[192,1280]{1,0:T(8,128)(2,1)} %reshape.92), channel_id=1, source_target_pairs={{0,1},{1,0},{2,3},{3,2},{4,5},{5,4},{6,7},{7,6},{8,9},{9,8},{10,11... | collective-permute-start | bytes 1474568 | tf_op jit(solution)/shard_map/ppermute | solution.py:20
  95.2 8.9 %copy-start.15 = (bf16[1,1280,1280]{2,1,0:T(8,128)(2,1)S(1)}, bf16[1,1280,1280]{2,1,0:T(8,128)(2,1)}, u32[]{:S(2)}) copy-start(bf16[1,1280,1280]{2,1,0:T(8,128)(2,1)} %param.11) | copy-start | bytes 9830404
  96.7 9.6 %copy-start.17 = (f32[384,1280]{1,0:T(8,128)}, f32[384,1280]{1,0:T(8,128)S(1)}, u32[]{:S(2)}) copy-start(f32[384,1280]{1,0:T(8,128)S(1)} %fusion.22) | copy-start | bytes 5898244
  104.1 2.1 copy-start.9
  106.2 1.0 copy-start.19
  110.9 5.0 %copy-start.16 = (bf16[1,1280,1280]{2,1,0:T(8,128)(2,1)S(1)}, bf16[1,1280,1280]{2,1,0:T(8,128)(2,1)}, u32[]{:S(2)}) copy-start(bf16[1,1280,1280]{2,1,0:T(8,128)(2,1)} %param.11) | copy-start | bytes 9830404
  110.9 5.0 %copy-start.18 = (f32[384,1280]{1,0:T(8,128)S(1)}, f32[384,1280]{1,0:T(8,128)}, u32[]{:S(2)}) copy-start(f32[384,1280]{1,0:T(8,128)} %copy-done.17) | copy-start | bytes 5898244
  113.8 28.7 %collective-permute-start.3 = (bf16[192,1280]{1,0:T(8,128)(2,1)S(1)}, bf16[192,1280]{1,0:T(8,128)(2,1)S(1)}, u32[]{:S(2)}, u32[]{:S(2)}) collective-permute-start(bf16[192,1280]{1,0:T(8,128)(2,1)S(1)} %slice.59), channel_id=1, source_target_pairs={{0,1},{1,0},{2,3},{3,2},{4,5},{5,4},{6,7},{7,6},{8,9},{9,8},{10,11... | collective-permute-start | bytes 1474568 | tf_op jit(solution)/shard_map/ppermute | solution.py:20
  117.7 1.3 copy-start.4
  119.9 54.9 %collective-permute-start.1 = (bf16[192,1280]{1,0:T(8,128)(2,1)}, bf16[192,1280]{1,0:T(8,128)(2,1)}, u32[]{:S(2)}, u32[]{:S(2)}) collective-permute-start(bf16[192,1280]{1,0:T(8,128)(2,1)} %slice.60), channel_id=1, source_target_pairs={{0,1},{1,0},{2,3},{3,2},{4,5},{5,4},{6,7},{7,6},{8,9},{9,8},{10,11... | collective-permute-start | bytes 1474568 | tf_op jit(solution)/shard_map/ppermute | solution.py:20
  145.5 33.5 %all-to-all-start.3 = ((bf16[96,1,2,1280]{3,2,1,0:T(2,128)(2,1)}), bf16[96,1,2,1280]{3,2,1,0:T(2,128)(2,1)}, u32[]{:S(2)}, u32[]{:S(2)}) async-start(bf16[96,1,2,1280]{3,2,1,0:T(2,128)(2,1)} %bitcast.172), calls=%async_computation.3 | async-start | bytes 983040 | tf_op jit(solution)/shard_map/all_to_all | solution.py:106
  153.0 126.0 %reduce-scatter.5.cloned.1.call-start = ((), (), s32[]{:S(2)}) async-start(), calls=%async_computation.10 | async-start | bytes 3686400 | tf_op jit(solution)/shard_map/reduce_scatter | solution.py:118
  178.9 24.6 %all-to-all-start.1 = ((bf16[96,1,2,1280]{3,2,1,0:T(2,128)(2,1)}), bf16[96,1,2,1280]{3,2,1,0:T(2,128)(2,1)}, u32[]{:S(2)}, u32[]{:S(2)}) async-start(bf16[96,1,2,1280]{3,2,1,0:T(2,128)(2,1)} %bitcast.173), calls=%async_computation.1 | async-start | bytes 983040 | tf_op jit(solution)/shard_map/all_to_all | solution.py:106
  203.5 7.8 %copy-start.10 = (f32[6,256,32]{1,2,0:T(8,128)S(1)}, f32[6,256,32]{1,2,0:T(8,128)}, u32[]{:S(2)}) copy-start(f32[6,256,32]{1,2,0:T(8,128)} %get-tuple-element.18) | copy-start | bytes 589828
  207.7 4.0 %copy-start.2 = (bf16[6,256,1280]{2,1,0:T(8,128)(2,1)S(1)}, bf16[6,256,1280]{2,1,0:T(8,128)(2,1)}, u32[]{:S(2)}) copy-start(bf16[6,256,1280]{2,1,0:T(8,128)(2,1)} %param.6) | copy-start | bytes 11796484
  207.7 4.0 %copy-start.3 = (bf16[6,32,1280]{2,1,0:T(8,128)(2,1)S(1)}, bf16[6,32,1280]{2,1,0:T(8,128)(2,1)}, u32[]{:S(2)}) copy-start(bf16[6,32,1280]{2,1,0:T(8,128)(2,1)} %reshape.94) | copy-start | bytes 1474564
  211.7 1.5 copy-start.6
  214.2 1.6 copy-start.20
  214.2 1.6 copy-start.21
  220.3 13.3 %all-to-all-start.4 = ((f32[16,24,128]{2,1,0:T(8,128)}), f32[16,24,128]{2,1,0:T(8,128)S(1)}, u32[]{:S(2)}, u32[]{:S(2)}) async-start(f32[16,24,128]{2,1,0:T(8,128)} %bitcast.175), calls=%async_computation.4 | async-start | bytes 393216 | tf_op jit(solution)/shard_map/all_to_all | solution.py:69
  234.3 17.6 %all-to-all-start.5 = ((f32[16,24,128]{2,1,0:T(8,128)}), f32[16,24,128]{2,1,0:T(8,128)S(1)}, u32[]{:S(2)}, u32[]{:S(2)}) async-start(f32[16,24,128]{2,1,0:T(8,128)} %broadcast_in_dim.14), calls=%async_computation.5 | async-start | bytes 393216 | tf_op jit(solution)/shard_map/all_to_all | solution.py:14
  252.7 15.9 %all-to-all-start.6 = ((f32[16,24,128]{2,1,0:T(8,128)}), f32[16,24,128]{2,1,0:T(8,128)S(1)}, u32[]{:S(2)}, u32[]{:S(2)}) async-start(f32[16,24,128]{2,1,0:T(8,128)} %broadcast_in_dim.15), calls=%async_computation.6 | async-start | bytes 393216 | tf_op jit(solution)/shard_map/all_to_all | solution.py:14
  258.3 10.2 %copy-start.8 = (bf16[1280,32]{0,1:T(8,128)(2,1)S(1)}, bf16[1280,32]{0,1:T(8,128)(2,1)}, u32[]{:S(2)}) copy-start(bf16[1280,32]{0,1:T(8,128)(2,1)} %param.9) | copy-start | bytes 245764
Sparse Core Ops, SparseCore 0:
  111.1 90.7 reduce-scatter.2
  205.0 74.0 reduce-scatter.4
